TPU v7x, 32 devices: a whole 2x2x4 slice. The times are simulated.
32 devices in a mesh: gx: 2 (over x), gy: 4 (over z), gz: 4 (over y, core).
Axes of the slice: x: 2, y: 2, z: 4, core: 2. Of those that a mesh axis runs over, the one named last changes fastest.
Arguments:
- tokens: bfloat16 [512, 49, 512], P(('gx', 'gy', 'gz')), may hold values from -6 to 6
- cotangent: bfloat16 [512, 49, 512], P(('gx', 'gy', 'gz')), may hold values from -6 to 6
- regions: int32 [512, 49], P(('gx', 'gy', 'gz')), may hold values from 0 to 3
- rel_index: int32 [49, 49], replicated, may hold values from 0 to 168
- w_qkv: bfloat16 [512, 1536], replicated, may hold values from -0.25 to 0.25
- w_proj: bfloat16 [512, 512], replicated, may hold values from -0.25 to 0.25
- bias_table: float32 [169, 16], replicated, may hold values from -4 to 4
- mom_qkv: float32 [786432], P(('gx', 'gy', 'gz')), may hold values from -0.06 to 0.06
- mom_proj: float32 [262144], P(('gx', 'gy', 'gz')), may hold values from -0.06 to 0.06
- mom_table: float32 [169, 16], replicated, may hold values from -0.06 to 0.06
Outputs:
- new_mom_qkv: float32 [786432], P(('gx', 'gy', 'gz'))
- new_mom_proj: float32 [262144], P(('gx', 'gy', 'gz'))
- new_mom_table: float32 [169, 16], replicated
All inputs are finite; a program needn't handle non-finite values.
Results may differ from a plain program's by a relative error of at most 0.015.
Values sent between devices are 32-bit elements; how exact they have to be, the bound alone decides.
A program may use at most 128 MiB of HBM per device.

v0:
```python
import functools
import math

import jax
import jax.numpy as jnp
from jax import lax
from jax.experimental import pallas as pl
from jax.experimental.pallas import tpu as pltpu
from jax.sharding import PartitionSpec as P

AXES = ("gx", "gy", "gz")
MESH = pl.DeviceIdType.MESH
F32, BF16 = jnp.float32, jnp.bfloat16
PAD = 64
GROUP = 4
LOG2E = math.log2(math.e)
STEPS = 5
NT = (((1,), (1,)), ((), ()))
TN = (((0,), (0,)), ((), ()))


def dot(a, b, dims=(((1,), (0,)), ((), ()))):
    return lax.dot_general(a, b, dims, preferred_element_type=F32)


def spread(value, lanes, width):
    return jnp.concatenate(
        [jnp.where(lanes // width == h, value, jnp.zeros_like(value)) for h in range(GROUP)], axis=0
    )


def gather_heads(value, lanes, width):
    total = jnp.where(lanes // width == 0, value[:PAD], 0.0)
    for h in range(1, GROUP):
        total = jnp.where(lanes // width == h, value[h * PAD : (h + 1) * PAD], total)
    return total


class Exchange:
    def __init__(self, grad, recvs, send_sem, recv_sem, chunk, where):
        self.grad, self.recvs, self.send_sem, self.recv_sem = grad, recvs, send_sem, recv_sem
        self.chunk, self.where, self.step = chunk, where, 0

    def copy(self, half, step):
        bits, partners = self.where[half]
        src = self.grad.at[(half, *bits[:step], 1 - bits[step])]
        return pltpu.make_async_remote_copy(
            src_ref=src,
            dst_ref=self.recvs[step].at[half],
            send_sem=self.send_sem.at[self.chunk, half, step],
            recv_sem=self.recv_sem.at[self.chunk, half, step],
            device_id=partners[step],
            device_id_type=MESH,
        )

    def start(self):
        for half in range(2):
            self.copy(half, 0).start()

    def advance(self):
        step = self.step
        if step >= STEPS:
            return
        for half in range(2):
            self.copy(half, step).wait()
            bits = self.where[half][0]
            at = (half, *bits[: step + 1])
            self.grad[at] = self.grad[at] + self.recvs[step][half]
            if step + 1 < STEPS:
                self.copy(half, step + 1).start()
        self.step += 1


def kernel(dims, *refs):
    win, count, dim, heads, entries, remote = dims
    width = dim // heads
    groups = heads // GROUP
    scale = width**-0.5
    tok, cot, reg, rel, w_qkv, w_proj, table = refs[:7]
    rest = refs[7:]
    if remote:
        out, out_table = rest[:2]
        rest = rest[2:]
    else:
        out_qkv, out_proj, out_table = rest[:3]
        rest = rest[3:]
    x, xt, c, qkv, d_att, att, d_qkv, probs, masks, bias, bias_rows, d_bias, small, rel_t, tab = rest[:15]
    rest = rest[15:]
    if remote:
        tab_buf, tab_recv, tab_send, tab_sem, send_sem, recv_sem, grad_p, grad_q = rest[:8]
        recv_p, recv_q = rest[8 : 8 + STEPS], rest[8 + STEPS : 8 + 2 * STEPS]
        gx, gy, gz = (lax.axis_index(a) for a in AXES)
        core, ypos, z0, z1 = gz % 2, gz // 2, gy % 2, gy // 2
        to_core = (gx, gy, gz + 1 - 2 * core)
        to_x = (1 - gx, gy, gz)
        to_y = (gx, gy, gz + 2 - 4 * ypos)
        to_z0 = (gx, gy + 1 - 2 * z0, gz)
        to_z1 = (gx, gy + 2 - 4 * z1, gz)
        where = (
            ((core, gx, ypos, z0, z1), (to_core, to_x, to_y, to_z0, to_z1)),
            ((core, ypos, gx, z0, z1), (to_core, to_y, to_x, to_z0, to_z1)),
        )
        barrier = pltpu.get_barrier_semaphore()
        for there in where[0][1]:
            pl.semaphore_signal(barrier, inc=1, device_id=there, device_id_type=MESH)
        pl.semaphore_wait(barrier, STEPS)

    lanes = lax.broadcasted_iota(jnp.int32, (PAD, GROUP * width), 1)

    x[...] = jnp.zeros_like(x)
    c[...] = jnp.zeros_like(c)
    for w in range(win):
        x[pl.ds(w * PAD, count), :] = tok[w]
        c[pl.ds(w * PAD, count), :] = cot[w]
    rows_all = win * PAD

    @pl.loop(0, rows_all // 256)
    def _(i):
        rows = pl.ds(pl.multiple_of(i * 256, 256), 256)
        qkv[rows, :] = dot(x[rows, :], w_qkv[...]).astype(BF16)
        d_att[rows, :] = dot(c[rows, :], w_proj[...], NT).astype(BF16)

    xt[...] = x[...].T

    small[...] = jnp.zeros_like(small)
    small[0:win, 0:count] = reg[...].astype(F32)
    reg_rows = small[...]
    reg_cols = reg_rows.T
    for w in range(win):
        row = reg_rows[w : w + 1, :PAD]
        row = jnp.concatenate([row, row], axis=1)
        masks[w * PAD : (w + 1) * PAD, :] = jnp.where(
            reg_cols[:PAD, w : w + 1] == row, 0.0, -100.0 * LOG2E
        )

    small[...] = jnp.full_like(small, -1.0)
    small[0:count, 0:count] = rel[...].astype(F32)
    rel_t[...] = small[...].T
    tab[...] = jnp.zeros_like(tab)
    tab[0:entries, 0:heads] = table[...]
    size = tab.shape[0]
    tab_t = tab[...].T[:heads]
    high = tab_t.astype(BF16)
    low = (tab_t - high.astype(F32)).astype(BF16)
    both = jnp.concatenate([high, low], axis=0)
    entry = lax.broadcasted_iota(jnp.int32, (size, 128), 0).astype(F32)

    def one_hot(j):
        return jnp.where(entry == rel_t[pl.ds(j, 1), :], 1.0, 0.0).astype(BF16)

    bias_rows[...] = jnp.full_like(bias_rows, -1e30)

    def look(j, carry):
        found = dot(both, one_hot(j))
        bias_rows[pl.ds(pl.multiple_of(j * heads, heads), heads), :] = (
            found[:heads] + found[heads:]
        ) * LOG2E
        return carry

    lax.fori_loop(0, count, look, 0)
    for g in range(groups):
        bias[g] = jnp.concatenate(
            [bias_rows[pl.ds(g * GROUP + h, PAD, stride=heads), :][:, :PAD] for h in range(GROUP)],
            axis=1,
        )
    d_bias[...] = jnp.zeros_like(d_bias)

    def rows_of(w):
        at = w * PAD
        return pl.ds(at if isinstance(at, int) else pl.multiple_of(at, PAD), PAD)

    def part(ref, which, g, rows):
        at = which * dim + g * GROUP * width
        return ref[rows, at : at + GROUP * width]

    def forward(w, carry):
        rows = rows_of(w)
        mask = masks[rows, :]
        mask = jnp.concatenate([mask] * (GROUP * PAD // 128), axis=1)
        every = range(groups)
        queries = [spread(part(qkv, 0, g, rows), lanes, width) for g in every]
        scores = [dot(part(qkv, 1, g, rows), queries[g], NT) for g in every]
        scores = [scores[g] * (scale * LOG2E) + bias[g] + mask for g in every]
        raised = [jnp.exp2(v - jnp.max(v, axis=0, keepdims=True)) for v in scores]
        p = [(v * (1.0 / jnp.sum(v, axis=0, keepdims=True))).astype(BF16) for v in raised]
        mixed = [dot(p[g], part(qkv, 2, g, rows), TN) for g in every]
        joined = [gather_heads(v, lanes, width).astype(BF16) for v in mixed]
        att[rows, :] = jnp.concatenate(joined, axis=1)
        for g in every:
            probs[g, rows, :] = p[g]
        return carry

    lax.fori_loop(0, win, forward, 0)

    def place(value, ref):
        for d in range(value.shape[0] // 16):
            dx, dy, dz = d // 16, (d // 4) % 4, d % 4
            for half in range(2):
                a, b = (dx, dz // 2) if half == 0 else (dz // 2, dx)
                block = value[16 * d + 8 * half : 16 * d + 8 * half + 8]
                ref[half, dz % 2, a, b, dy % 2, dy // 2] = block

    g_proj = dot(att[...], c[...], TN)
    active = []
    if remote:
        place(g_proj, grad_p)
        active.append(Exchange(grad_p, recv_p, send_sem, recv_sem, 0, where))
        active[0].start()
    else:
        out_proj[...] = g_proj

    def backward(g, windows):
        rows = [rows_of(w) for w in windows]
        queries = [spread(part(qkv, 0, g, r), lanes, width) for r in rows]
        d_out = [spread(part(d_att, 0, g, r), lanes, width) for r in rows]
        p = [probs[g, r, :] for r in rows]
        every = range(len(rows))
        d_probs = [dot(part(qkv, 2, g, rows[n]), d_out[n], NT) for n in every]
        d_v = [dot(p[n], d_out[n]) for n in every]
        pf = [v.astype(F32) for v in p]
        weighted = [pf[n] * d_probs[n] for n in every]
        d_scores = [
            weighted[n] - pf[n] * jnp.sum(weighted[n], axis=0, keepdims=True) for n in every
        ]
        d_bias[g] += sum(d_scores[1:], d_scores[0])
        ds = [v.astype(BF16) for v in d_scores]
        d_k = [dot(ds[n], queries[n]) * scale for n in every]
        d_q = [dot(ds[n], part(qkv, 1, g, rows[n]), TN) for n in every]
        d_q = [gather_heads(v, lanes, width) * scale for v in d_q]
        for n in every:
            d_qkv[rows[n], :] = jnp.concatenate([d_q[n], d_k[n], d_v[n]], axis=1).astype(BF16)

    pieces = 4
    wide = GROUP * width
    for g in range(groups):
        for s in range(pieces):
            backward(g, range(s * win // pieces, (s + 1) * win // pieces))
            for each in active:
                each.advance()
        g_qkv = dot(xt[...], d_qkv[...])
        if remote:
            place(g_qkv, grad_q.at[g])
            active.append(Exchange(grad_q.at[g], [r.at[g] for r in recv_q], send_sem, recv_sem, g + 1, where))
            active[-1].start()
        else:
            for which in range(3):
                at = which * dim + g * wide
                out_qkv[:, at : at + wide] = g_qkv[:, which * wide : (which + 1) * wide]

    for each in active:
        each.advance()

    for g in range(groups):
        for h in range(GROUP):
            piece = d_bias[g, :, h * PAD : (h + 1) * PAD]
            bias_rows[pl.ds(g * GROUP + h, PAD, stride=heads), :] = jnp.concatenate(
                [piece, jnp.zeros_like(piece)], axis=1
            )

    def collect(j, total):
        value = bias_rows[pl.ds(pl.multiple_of(j * heads, heads), heads), :]
        top = value.astype(BF16)
        rest_of = (value - top.astype(F32)).astype(BF16)
        return total + dot(jnp.concatenate([top, rest_of], axis=0), one_hot(j), NT)

    g_table = lax.fori_loop(0, count, collect, jnp.zeros((2 * heads, size), F32))
    g_table = g_table[:heads] + g_table[heads:]
    if not remote:
        out_table[...] = g_table
        return

    tab_buf[0] = g_table
    for step in range(STEPS):
        sent = pltpu.make_async_remote_copy(
            src_ref=tab_buf.at[step],
            dst_ref=tab_recv.at[step],
            send_sem=tab_send.at[step],
            recv_sem=tab_sem.at[step],
            device_id=where[0][1][step],
            device_id_type=MESH,
        )
        sent.start()
        for each in active:
            each.advance()
        sent.wait()
        tab_buf[step + 1] = tab_buf[step] + tab_recv[step]
    for each in active:
        while each.step < STEPS:
            each.advance()
    out_table[...] = tab_buf[STEPS]
    for half in range(2):
        bits = where[half][0]
        rows = pl.ds(8 * half, 8)
        out[rows, 3 * dim :] = grad_p[(half, *bits)]
        for g in range(groups):
            done = grad_q[(g, half, *bits)]
            for which in range(3):
                at = which * dim + g * wide
                out[rows, at : at + wide] = done[:, which * wide : (which + 1) * wide]


def local_grads(remote, tokens, cotangent, regions, rel_index, w_qkv, w_proj, bias_table):
    win, count, dim = tokens.shape
    entries, heads = bias_table.shape
    groups = heads // GROUP
    rows = win * PAD
    wide = GROUP * (dim // heads)
    size = -(-entries // 128) * 128
    scratch = [
        pltpu.VMEM((rows, dim), BF16),
        pltpu.VMEM((dim, rows), BF16),
        pltpu.VMEM((rows, dim), BF16),
        pltpu.VMEM((rows, 3 * dim), BF16),
        pltpu.VMEM((rows, dim), BF16),
        pltpu.VMEM((rows, dim), BF16),
        pltpu.VMEM((rows, 3 * wide), BF16),
        pltpu.VMEM((groups, rows, GROUP * PAD), BF16),
        pltpu.VMEM((rows, 128), F32),
        pltpu.VMEM((groups, PAD, GROUP * PAD), F32),
        pltpu.VMEM((PAD * heads, 128), F32),
        pltpu.VMEM((groups, PAD, GROUP * PAD), F32),
        pltpu.VMEM((128, 128), F32),
        pltpu.VMEM((128, 128), F32),
        pltpu.VMEM((size, 128), F32),
    ]
    if remote:
        outs = ((dim // lax.axis_size(AXES), 4 * dim), (heads, size))
        scratch += [
            pltpu.VMEM((STEPS + 1, heads, size), F32),
            pltpu.VMEM((STEPS, heads, size), F32),
            pltpu.SemaphoreType.DMA((STEPS,)),
            pltpu.SemaphoreType.DMA((STEPS,)),
            pltpu.SemaphoreType.DMA((groups + 1, 2, STEPS)),
            pltpu.SemaphoreType.DMA((groups + 1, 2, STEPS)),
            pltpu.VMEM((2,) + (2,) * STEPS + (8, dim), F32),
            pltpu.VMEM((groups, 2) + (2,) * STEPS + (8, 3 * wide), F32),
        ]
        for step in range(STEPS):
            scratch.append(pltpu.VMEM((2,) + (2,) * (STEPS - 1 - step) + (8, dim), F32))
        for step in range(STEPS):
            scratch.append(
                pltpu.VMEM((groups, 2) + (2,) * (STEPS - 1 - step) + (8, 3 * wide), F32)
            )
        params = dict(collective_id=0, has_side_effects=True)
    else:
        outs = ((dim, 3 * dim), (dim, dim), (heads, size))
        params = dict()
    dims = (win, count, dim, heads, entries, remote)
    vmem = pl.BlockSpec(memory_space=pltpu.VMEM)
    return pl.pallas_call(
        functools.partial(kernel, dims),
        out_shape=[jax.ShapeDtypeStruct(o, F32) for o in outs],
        in_specs=[vmem] * 7,
        out_specs=[vmem] * len(outs),
        scratch_shapes=scratch,
        compiler_params=pltpu.CompilerParams(vmem_limit_bytes=60 * 1024 * 1024, **params),
    )(tokens, cotangent, regions, rel_index, w_qkv, w_proj, bias_table)


def body(
    tokens, cotangent, regions, rel_index, w_qkv, w_proj, bias_table, mom_qkv, mom_proj, mom_table
):
    dim = tokens.shape[2]
    entries = bias_table.shape[0]
    devices = lax.axis_size(AXES)
    sizes = tuple(lax.axis_size(a) for a in AXES)
    scale = 1.0 / (tokens.shape[0] * devices)
    args = (tokens, cotangent, regions, rel_index, w_qkv, w_proj, bias_table)
    if sizes == (2, 4, 4) and dim == 16 * devices:
        mine, table = local_grads(True, *args)
        qkv_mine, proj_mine = mine[:, : 3 * dim].reshape(-1), mine[:, 3 * dim :].reshape(-1)
    else:
        qkv, proj, table = local_grads(False, *args)
        qkv_mine = lax.psum_scatter(qkv.reshape(-1), AXES, tiled=True)
        proj_mine = lax.psum_scatter(proj.reshape(-1), AXES, tiled=True)
        table = lax.psum(table, AXES)
    return (
        0.9 * mom_qkv + qkv_mine * scale,
        0.9 * mom_proj + proj_mine * scale,
        0.9 * mom_table + table[:, :entries].T * scale,
    )


def solution(mesh):
    return jax.shard_map(
        body,
        mesh=mesh,
        in_specs=(
            P(AXES, None, None),
            P(AXES, None, None),
            P(AXES, None),
            P(),
            P(),
            P(),
            P(),
            P(AXES),
            P(AXES),
            P(),
        ),
        out_specs=(P(AXES), P(AXES), P()),
        check_vma=False,
    )
```

profile of v0, /device:TPU:0, one launch (start us, length us, event | category | flops | bytes accessed | tf_op | source)
XLA Modules:
  0.0 115.2 jit_solution(11571482934375317902)
XLA Ops:
  0.6 0.0 copy-start
  0.6 1.5 %copy.15.refs_6_ = f32[169,16]{1,0:T(8,128)} copy(f32[169,16]{0,1:T(8,128)} %param.16) | data formatting | bytes 21632 | tf_op args[6]
  2.2 2.5 %copy.13.refs_0_ = bf16[16,49,512]{2,1,0:T(8,128)(2,1)} copy(bf16[16,49,512]{2,0,1:T(8,128)(2,1)} %param.10) | data formatting | bytes 1605632 | tf_op args[0]
  4.7 0.0 copy-done
  4.7 1.4 %copy.14.refs_1_ = bf16[16,49,512]{2,1,0:T(8,128)(2,1)} copy(bf16[16,49,512]{2,0,1:T(8,128)(2,1)S(1)} %copy-done) | data formatting | bytes 1605632 | tf_op args[1]
  6.1 0.0 copy-start.3
  6.1 0.0 copy-start.1
  6.1 0.0 copy-start.2
  6.1 104.7 %shard_map.121 = (f32[16,2048]{1,0:T(8,128)}, f32[16,256]{1,0:T(8,128)}) custom-call(bf16[16,49,512]{2,1,0:T(8,128)(2,1)} %copy.13.refs_0_, bf16[16,49,512]{2,1,0:T(8,128)(2,1)} %copy.14.refs_1_, s32[16,49]{1,0:T(8,128)} %refs_2_.1, s32[49,49]{1,0:T(8,128)} %refs_3_.1, bf16[512,1536]{1,0:T(8,128)(2,1)} %refs_4_.1, bf16[512,512]{1,0:T(8,128)(2,1)} %refs_5_.1, ...), custom_call_target="tpu_custom_call" | custom-call | tf_op jit(solution)/shard_map/pallas_call | solution.py:350
  110.8 0.0 copy-done.3
  110.8 1.3 %bitcast_add_fusion = f32[169,16]{0,1:T(8,128)} fusion(f32[16,256]{1,0:T(8,128)} %get-tuple-element.6, f32[169,16]{0,1:T(8,128)S(1)} %copy-done.3), kind=kLoop, calls=%fused_computation.4 | loop fusion | flops 8112 | bytes 32448 | tf_op jit(solution)/shard_map/add | solution.py:380
  112.2 0.8 multiply_bitcast_fusion
  112.9 0.9 slice_multiply_fusion
  113.8 0.0 copy-done.1
  113.8 0.7 multiply_add_fusion
  114.5 0.0 copy-done.2
  114.5 0.6 multiply_add_fusion.1
  (2 shorter events, 0.0 us)
Async XLA Ops:
  0.6 4.1 %copy-start = (bf16[16,49,512]{2,0,1:T(8,128)(2,1)S(1)}, bf16[16,49,512]{2,0,1:T(8,128)(2,1)}, u32[]{:S(2)}) copy-start(bf16[16,49,512]{2,0,1:T(8,128)(2,1)} %param.11) | copy-start | bytes 2408452
  6.1 104.7 %copy-start.3 = (f32[169,16]{0,1:T(8,128)S(1)}, f32[169,16]{0,1:T(8,128)}, u32[]{:S(2)}) copy-start(f32[169,16]{0,1:T(8,128)} %param.19) | copy-start | bytes 32452
  6.1 107.8 %copy-start.1 = (f32[24576]{0:T(1024)S(1)}, f32[24576]{0:T(1024)}, u32[]{:S(2)}) copy-start(f32[24576]{0:T(1024)} %param.17) | copy-start | bytes 294916
  6.1 108.4 %copy-start.2 = (f32[8192]{0:T(1024)S(1)}, f32[8192]{0:T(1024)}, u32[]{:S(2)}) copy-start(f32[8192]{0:T(1024)} %param.18) | copy-start | bytes 98308
where the time goes:
time: 116 us; the launch traced here: 115 us
  Pallas kernels  105 us (91%)
  local copies, waits for them, and re-layouts  5.48 us (5%)
  other arithmetic  4.27 us (4%)
    pallas_call x1, Pallas kernels, local_grads(): pl.pallas_call(functools.partial(kernel, dims), out_shape=[jax.ShapeDtype...  105 us
    unnamed x12, local copies, waits for them, and re-layouts  5.47 us

commit v1 on v0

v1 whole, which is shorter than its diff:
```python
import functools
import math

import jax
import jax.numpy as jnp
from jax import lax
from jax.experimental import pallas as pl
from jax.experimental.pallas import tpu as pltpu
from jax.sharding import PartitionSpec as P

AXES = ("gx", "gy", "gz")
MESH = pl.DeviceIdType.MESH
F32, BF16 = jnp.float32, jnp.bfloat16
PAD = 64
GROUP = 4
LOG2E = math.log2(math.e)
NT = (((1,), (1,)), ((), ()))
TN = (((0,), (0,)), ((), ()))
COPIES = 8
DUE = (3, 6, 5, 7)


def dot(a, b, dims=(((1,), (0,)), ((), ()))):
    return lax.dot_general(a, b, dims, preferred_element_type=F32)


def spread(value, lanes, width):
    return jnp.concatenate(
        [jnp.where(lanes // width == h, value, jnp.zeros_like(value)) for h in range(GROUP)], axis=0
    )


def gather_heads(value, lanes, width):
    total = jnp.where(lanes // width == 0, value[:PAD], 0.0)
    for h in range(1, GROUP):
        total = jnp.where(lanes // width == h, value[h * PAD : (h + 1) * PAD], total)
    return total


class Place:
    def __init__(self):
        gx, gy, gz = (lax.axis_index(a) for a in AXES)
        self.x, self.z = gx, gy
        self.core, self.y = gz % 2, gz // 2
        self.to_core = (gx, gy, gz + 1 - 2 * self.core)
        self.to_x = (1 - gx, gy, gz)
        self.to_y = (gx, gy, gz + 2 - 4 * self.y)
        self.to_xy = (1 - gx, gy, gz + 2 - 4 * self.y)
        self.others = [(gy + k) % 4 for k in range(1, 4)]
        self.to_z = [(gx, there, gz) for there in self.others]

    def everyone(self):
        return [self.to_core, self.to_x, self.to_y, self.to_xy, *self.to_z]


class Chunk:
    def __init__(self, place, refs, send, recv, due, finish):
        self.p = place
        self.buf, self.r0, self.r1, self.r2, self.s2, self.r3 = refs
        self.send, self.recv, self.finish = send, recv, finish
        self.ab = ((place.x, place.y), (place.y, place.x))
        self.via = ((place.to_x, place.to_y), (place.to_y, place.to_x))
        self.stage, self.due = 0, due

    def copy(self, n, src, dst, there):
        return pltpu.make_async_remote_copy(
            src_ref=src,
            dst_ref=dst,
            send_sem=self.send.at[n],
            recv_sem=self.recv.at[n],
            device_id=there,
            device_id_type=MESH,
        )

    def copies(self, stage):
        p, buf = self.p, self.buf
        if stage == 0:
            return [self.copy(0, buf.at[1 - p.core], self.r0, p.to_core)]
        if stage == 1:
            return [
                self.copy(1 + h, buf.at[p.core, h, 1 - self.ab[h][0]], self.r1.at[h], self.via[h][0])
                for h in range(2)
            ]
        if stage == 2:
            return [
                self.copy(
                    3 + h,
                    buf.at[p.core, h, self.ab[h][0], 1 - self.ab[h][1]],
                    self.r2.at[h],
                    self.via[h][1],
                )
                for h in range(2)
            ]
        return [self.copy(5 + k, self.s2.at[p.others[k]], self.r3.at[k], p.to_z[k]) for k in range(3)]

    def start(self):
        for c in self.copies(0):
            c.start()

    def advance(self):
        p, buf, stage = self.p, self.buf, self.stage
        waited = self.copies(stage)
        after = self.copies(stage + 1) if stage < 3 else []
        if stage == 0:
            waited[0].wait()
            for h in range(2):
                away = 1 - self.ab[h][0]
                at = (p.core, h, away)
                buf[at] = buf[at] + self.r0[h, away]
                after[h].start()
        elif stage == 1:
            for h in range(2):
                a, b = self.ab[h]
                waited[h].wait()
                at = (p.core, h, a, 1 - b)
                buf[at] = buf[at] + self.r0[h, a, 1 - b] + self.r1[h, 1 - b]
                after[h].start()
        elif stage == 2:
            for h in range(2):
                a, b = self.ab[h]
                waited[h].wait()
                self.s2[:, h] = (
                    buf[p.core, h, a, b] + self.r0[h, a, b] + self.r1[h, b] + self.r2[h]
                )
            for c in after:
                c.start()
        else:
            for c in waited:
                c.wait()
            self.finish(self.s2[p.z] + self.r3[0] + self.r3[1] + self.r3[2])
        self.stage += 1


class Table:
    def __init__(self, place, refs, send, recv, due, finish):
        self.p = place
        self.t0, self.r0, self.t1, self.r1, self.r2 = refs
        self.send, self.recv, self.finish = send, recv, finish
        self.stage, self.due = 1, due

    def copy(self, n, src, dst, there):
        return pltpu.make_async_remote_copy(
            src_ref=src,
            dst_ref=dst,
            send_sem=self.send.at[n],
            recv_sem=self.recv.at[n],
            device_id=there,
            device_id_type=MESH,
        )

    def copies(self, stage):
        p = self.p
        if stage == 1:
            return [self.copy(0, self.t0, self.r0, p.to_core)]
        if stage == 2:
            return [
                self.copy(1 + k, self.t1, self.r1.at[k], there)
                for k, there in enumerate((p.to_x, p.to_y, p.to_xy))
            ]
        return [self.copy(4 + k, self.r2.at[p.z], self.r2.at[p.z], p.to_z[k]) for k in range(3)]

    def start(self):
        for c in self.copies(1):
            c.start()

    def advance(self):
        for c in self.copies(self.stage):
            if self.stage < 3:
                c.wait()
            else:
                c.wait_send()
        if self.stage == 1:
            self.t1[...] = self.t0[...] + self.r0[...]
        elif self.stage == 2:
            self.r2[self.p.z] = (self.t1[...] + self.r1[0]) + (self.r1[1] + self.r1[2])
        else:
            for k in range(3):
                there = (self.p.z + 3 - k) % 4
                self.copy(4 + k, self.r2.at[there], self.r2.at[there], self.p.to_z[k]).wait_recv()
            self.finish((self.r2[0] + self.r2[1]) + (self.r2[2] + self.r2[3]))
        if self.stage < 3:
            for c in self.copies(self.stage + 1):
                c.start()
        self.stage += 1


def kernel(dims, names, *all_refs):
    win, count, dim, heads, entries, remote, norm = dims
    r = dict(zip(names, all_refs, strict=True))
    width = dim // heads
    groups = heads // GROUP
    wide = GROUP * width
    scale = width**-0.5
    x, xt, c, qkv, d_att, att = r["x"], r["xt"], r["c"], r["qkv"], r["d_att"], r["att"]
    d_v, d_qk, probs, masks = r["d_v"], r["d_qk"], r["probs"], r["masks"]
    bias, bias_rows, d_bias, small, rel_t, tab = (
        r[n] for n in ("bias", "bias_rows", "d_bias", "small", "rel_t", "tab")
    )
    fetched = [("tok", "tok_v"), ("w_qkv", "w_qkv_v"), ("cot", "cot_v"), ("w_proj", "w_proj_v")]
    fetch = [
        pltpu.make_async_copy(r[a], r[b], r["fetch"].at[n]) for n, (a, b) in enumerate(fetched)
    ]
    for f in fetch:
        f.start()
    w_qkv, w_proj = r["w_qkv_v"], r["w_proj_v"]

    if remote:
        place = Place()
        barrier = pltpu.get_barrier_semaphore()
        for there in place.everyone():
            pl.semaphore_signal(barrier, inc=1, device_id=there, device_id_type=MESH)

    lanes = lax.broadcasted_iota(jnp.int32, (PAD, wide), 1)

    small[...] = jnp.zeros_like(small)
    small[0:win, 0:count] = r["reg"][...].astype(F32)
    reg_rows = small[...]
    reg_cols = reg_rows.T
    for w in range(win):
        row = reg_rows[w : w + 1, :PAD]
        row = jnp.concatenate([row, row], axis=1)
        masks[w * PAD : (w + 1) * PAD, :] = jnp.where(
            reg_cols[:PAD, w : w + 1] == row, 0.0, -100.0 * LOG2E
        )

    small[...] = jnp.full_like(small, -1.0)
    small[0:count, 0:count] = r["rel"][...].astype(F32)
    rel_t[...] = small[...].T
    tab[...] = jnp.zeros_like(tab)
    tab[:, 0:entries] = r["table"][...]
    size = tab.shape[1]
    tab_t = tab[...]
    high = tab_t.astype(BF16)
    low = (tab_t - high.astype(F32)).astype(BF16)
    both = jnp.concatenate([high, low], axis=0)
    entry = lax.broadcasted_iota(jnp.int32, (size, 128), 0).astype(F32)
    unroll = next(u for u in (7, 8, 4, 2, 1) if count % u == 0)

    def one_hot(j):
        return jnp.where(entry == rel_t[pl.ds(j, 1), :], 1.0, 0.0).astype(BF16)

    bias_rows[...] = jnp.full_like(bias_rows, -1e30)

    def look(i, carry):
        for u in range(unroll):
            j = i * unroll + u
            found = dot(both, one_hot(j))
            bias_rows[pl.ds(pl.multiple_of(j * heads, heads), heads), :] = (
                found[:heads] + found[heads:]
            ) * LOG2E
        return carry

    lax.fori_loop(0, count // unroll, look, 0)
    for g in range(groups):
        bias[g] = jnp.concatenate(
            [bias_rows[pl.ds(g * GROUP + h, PAD, stride=heads), :][:, :PAD] for h in range(GROUP)],
            axis=1,
        )
    d_bias[...] = jnp.zeros_like(d_bias)

    flat = r["flat"]
    rows_all = win * PAD
    for n in range(dim // 128):
        flat[n, count * win :, :] = jnp.zeros((rows_all - count * win, 128), F32)

    def by_window(src, dst):
        for n in range(dim // 128):
            cols = slice(n * 128, n * 128 + 128)
            for t in range(count):
                flat[n, t * win : (t + 1) * win, :] = src[t, :, cols].astype(F32)
            for w in range(win):
                dst[w * PAD : (w + 1) * PAD, cols] = flat[n, pl.ds(w, PAD, stride=win), :].astype(BF16)

    fetch[0].wait()
    by_window(r["tok_v"], x)
    fetch[2].wait()
    by_window(r["cot_v"], c)
    fetch[1].wait()
    fetch[3].wait()

    @pl.loop(0, rows_all // 256)
    def _(i):
        rows = pl.ds(pl.multiple_of(i * 256, 256), 256)
        qkv[rows, :] = dot(x[rows, :], w_qkv[...]).astype(BF16)
        d_att[rows, :] = dot(c[rows, :], w_proj[...], NT).astype(BF16)

    xt[...] = x[...].T

    def rows_of(w):
        at = w * PAD
        return pl.ds(at if isinstance(at, int) else pl.multiple_of(at, PAD), PAD)

    def part(ref, which, g, rows):
        at = which * dim + g * wide
        return ref[rows, at : at + wide]

    def forward(w, carry):
        rows = rows_of(w)
        mask = masks[rows, :]
        mask = jnp.concatenate([mask] * (GROUP * PAD // 128), axis=1)
        every = range(groups)
        queries = [spread(part(qkv, 0, g, rows), lanes, width) for g in every]
        d_out = [spread(part(d_att, 0, g, rows), lanes, width) for g in every]
        scores = [dot(part(qkv, 1, g, rows), queries[g], NT) for g in every]
        scores = [scores[g] * (scale * LOG2E) + bias[g] + mask for g in every]
        raised = [jnp.exp2(v - jnp.max(v, axis=0, keepdims=True)) for v in scores]
        p = [(v * (1.0 / jnp.sum(v, axis=0, keepdims=True))).astype(BF16) for v in raised]
        mixed = [dot(p[g], part(qkv, 2, g, rows), TN) for g in every]
        d_v[rows, :] = jnp.concatenate([dot(p[g], d_out[g]) for g in every], axis=1).astype(BF16)
        joined = [gather_heads(v, lanes, width).astype(BF16) for v in mixed]
        att[rows, :] = jnp.concatenate(joined, axis=1)
        for g in every:
            probs[g, rows, :] = p[g]
        return carry

    lax.fori_loop(0, win, forward, 0)

    tick = 0
    active = []

    def put(value, ref):
        for d in range(value.shape[0] // 16):
            dx, dz, dy, dc = d // 16, (d // 4) % 4, (d // 2) % 2, d % 2
            for half in range(2):
                a, b = (dx, dy) if half == 0 else (dy, dx)
                ref[dc, half, a, b, dz] = value[16 * d + 8 * half : 16 * d + 8 * half + 8]

    def update(out, mom, at, tiles, value):
        for half in range(2):
            for n in range(value.shape[2] // 128):
                rows = pl.ds(half * 8 * tiles + at(n), 8, stride=tiles)
                out[rows, :] = 0.9 * mom[rows, :] + value[half, :, n * 128 : n * 128 + 128] * norm

    def ship(name, n, value, finish):
        refs = [r[f"{name}_{k}"] for k in ("buf", "r0", "r1", "r2", "s2", "r3")]
        put(value, refs[0])
        chunk = Chunk(place, refs, r["send"].at[n], r["recv"].at[n], tick + DUE[0], finish)
        chunk.start()
        active.append(chunk)

    def run_due(limit):
        while True:
            ready = [k for k in active if k.stage < 4 and k.due <= limit]
            if not ready:
                return
            first = min(ready, key=lambda k: k.due)
            first.advance()
            if first.stage < 4:
                first.due += DUE[first.stage]

    if remote:
        pl.semaphore_wait(barrier, len(place.everyone()))
    tiles = dim // 128
    g_v = dot(xt[...], d_v[...])
    if remote:
        ship("v", 0, g_v, functools.partial(update, r["out_qkv"], r["mom_qkv"], lambda n: 2 * tiles + n, 3 * tiles))
    else:
        r["out_qkv"][:, 2 * dim :] = g_v
    g_proj = dot(att[...], c[...], TN)
    tick += 2
    if remote:
        ship("p", 1, g_proj, functools.partial(update, r["out_proj"], r["mom_proj"], lambda n: n, tiles))
    else:
        r["out_proj"][...] = g_proj

    def backward(g, windows):
        rows = [rows_of(w) for w in windows]
        queries = [spread(part(qkv, 0, g, rw), lanes, width) for rw in rows]
        d_out = [spread(part(d_att, 0, g, rw), lanes, width) for rw in rows]
        p = [probs[g, rw, :] for rw in rows]
        every = range(len(rows))
        d_probs = [dot(part(qkv, 2, g, rows[n]), d_out[n], NT) for n in every]
        pf = [v.astype(F32) for v in p]
        weighted = [pf[n] * d_probs[n] for n in every]
        d_scores = [
            weighted[n] - pf[n] * jnp.sum(weighted[n], axis=0, keepdims=True) for n in every
        ]
        d_bias[g] += sum(d_scores[1:], d_scores[0])
        ds = [v.astype(BF16) for v in d_scores]
        d_k = [dot(ds[n], queries[n]) * scale for n in every]
        d_q = [dot(ds[n], part(qkv, 1, g, rows[n]), TN) for n in every]
        d_q = [gather_heads(v, lanes, width) * scale for v in d_q]
        for n in every:
            d_qk[rows[n], :] = jnp.concatenate([d_q[n], d_k[n]], axis=1).astype(BF16)

    pieces = 4
    for g in range(groups):
        for s in range(pieces):
            backward(g, range(s * win // pieces, (s + 1) * win // pieces))
            tick += 1
            if remote:
                run_due(tick)
        g_qk = dot(xt[...], d_qk[...])
        tick += 1
        per = wide // 128
        if remote:
            at = lambda n, g=g: (n // per) * tiles + g * per + n % per
            ship(f"k{g}", 2 + g, g_qk, functools.partial(update, r["out_qkv"], r["mom_qkv"], at, 3 * tiles))
        else:
            for which in range(2):
                at = which * dim + g * wide
                r["out_qkv"][:, at : at + wide] = g_qk[:, which * wide : (which + 1) * wide]

    for g in range(groups):
        for h in range(GROUP):
            piece = d_bias[g, :, h * PAD : (h + 1) * PAD]
            bias_rows[pl.ds(g * GROUP + h, PAD, stride=heads), :] = jnp.concatenate(
                [piece, jnp.zeros_like(piece)], axis=1
            )

    def collect(i, total):
        for u in range(unroll):
            j = i * unroll + u
            value = bias_rows[pl.ds(pl.multiple_of(j * heads, heads), heads), :]
            top = value.astype(BF16)
            rest_of = (value - top.astype(F32)).astype(BF16)
            total = total + dot(jnp.concatenate([top, rest_of], axis=0), one_hot(j), NT)
        return total

    if remote:
        tick += 1
        run_due(tick)
    g_table = lax.fori_loop(0, count // unroll, collect, jnp.zeros((2 * heads, size), F32))
    g_table = g_table[:heads] + g_table[heads:]
    if not remote:
        r["out_table"][...] = g_table[:, :entries]
        return
    tick += 2
    refs = [r[f"t_{k}"] for k in ("t0", "r0", "t1", "r1", "r2")]
    refs[0][...] = g_table

    def table_done(value):
        r["out_table"][...] = 0.9 * r["mom_table"][...] + value[:, :entries] * norm

    last = Table(place, refs, r["send"].at[2 + groups], r["recv"].at[2 + groups], tick + 2, table_done)
    last.start()
    active.append(last)
    run_due(10**6)


def local_grads(remote, norm, tokens, cotangent, regions, rel_index, w_qkv, w_proj, bias_table, moms):
    win, count, dim = tokens.shape
    entries, heads = bias_table.shape
    groups = heads // GROUP
    rows = win * PAD
    wide = GROUP * (dim // heads)
    size = -(-entries // 128) * 128
    own = dim // 32
    inputs = dict(
        tok=tokens.transpose(1, 0, 2),
        cot=cotangent.transpose(1, 0, 2),
        reg=regions,
        rel=rel_index,
        w_qkv=w_qkv,
        w_proj=w_proj,
        table=bias_table.T,
    )
    if remote:
        inputs |= dict(
            mom_qkv=moms[0].reshape(-1, 128), mom_proj=moms[1].reshape(-1, 128), mom_table=moms[2].T
        )
        outs = dict(
            out_qkv=(own * 3 * dim // 128, 128), out_proj=(own * dim // 128, 128), out_table=(heads, entries)
        )
    else:
        outs = dict(out_qkv=(dim, 3 * dim), out_proj=(dim, dim), out_table=(heads, entries))
    vmem = pltpu.VMEM
    scratch = dict(
        fetch=pltpu.SemaphoreType.DMA((4,)),
        tok_v=vmem((count, win, dim), BF16),
        cot_v=vmem((count, win, dim), BF16),
        w_qkv_v=vmem((dim, 3 * dim), BF16),
        w_proj_v=vmem((dim, dim), BF16),
        flat=vmem((dim // 128, rows, 128), F32),
        x=vmem((rows, dim), BF16),
        xt=vmem((dim, rows), BF16),
        c=vmem((rows, dim), BF16),
        qkv=vmem((rows, 3 * dim), BF16),
        d_att=vmem((rows, dim), BF16),
        att=vmem((rows, dim), BF16),
        d_v=vmem((rows, dim), BF16),
        d_qk=vmem((rows, 2 * wide), BF16),
        probs=vmem((groups, rows, GROUP * PAD), BF16),
        masks=vmem((rows, 128), F32),
        bias=vmem((groups, PAD, GROUP * PAD), F32),
        bias_rows=vmem((PAD * heads, 128), F32),
        d_bias=vmem((groups, PAD, GROUP * PAD), F32),
        small=vmem((128, 128), F32),
        rel_t=vmem((128, 128), F32),
        tab=vmem((heads, size), F32),
    )
    params = dict()
    if remote:
        chunks = dict(v=dim, p=dim) | {f"k{g}": 2 * wide for g in range(groups)}
        for name, cols in chunks.items():
            scratch[f"{name}_buf"] = vmem((2, 2, 2, 2, 4, 8, cols), F32)
            scratch[f"{name}_r0"] = vmem((2, 2, 2, 4, 8, cols), F32)
            scratch[f"{name}_r1"] = vmem((2, 2, 4, 8, cols), F32)
            scratch[f"{name}_r2"] = vmem((2, 4, 8, cols), F32)
            scratch[f"{name}_s2"] = vmem((4, 2, 8, cols), F32)
            scratch[f"{name}_r3"] = vmem((3, 2, 8, cols), F32)
        for name, lead in dict(t0=(), r0=(), t1=(), r1=(3,), r2=(4,)).items():
            scratch[f"t_{name}"] = vmem((*lead, heads, size), F32)
        scratch["send"] = pltpu.SemaphoreType.DMA((len(chunks) + 1, COPIES))
        scratch["recv"] = pltpu.SemaphoreType.DMA((len(chunks) + 1, COPIES))
        params = dict(collective_id=0, has_side_effects=True)
    dims = (win, count, dim, heads, entries, remote, norm)
    spec = pl.BlockSpec(memory_space=pltpu.VMEM)
    where = {n: pl.BlockSpec(memory_space=pl.ANY) for n in ("tok", "cot", "w_qkv", "w_proj")}
    return pl.pallas_call(
        functools.partial(kernel, dims, [*inputs, *outs, *scratch]),
        out_shape=[jax.ShapeDtypeStruct(o, F32) for o in outs.values()],
        in_specs=[where.get(n, spec) for n in inputs],
        out_specs=[spec] * len(outs),
        scratch_shapes=list(scratch.values()),
        compiler_params=pltpu.CompilerParams(vmem_limit_bytes=60 * 1024 * 1024, **params),
    )(*inputs.values())


def body(
    tokens, cotangent, regions, rel_index, w_qkv, w_proj, bias_table, mom_qkv, mom_proj, mom_table
):
    dim = tokens.shape[2]
    devices = lax.axis_size(AXES)
    sizes = tuple(lax.axis_size(a) for a in AXES)
    norm = 1.0 / (tokens.shape[0] * devices)
    args = (tokens, cotangent, regions, rel_index, w_qkv, w_proj, bias_table)
    moms = (mom_qkv, mom_proj, mom_table)
    if sizes == (2, 4, 4) and dim == 16 * devices:
        qkv, proj, table = local_grads(True, norm, *args, moms)
        return qkv.reshape(-1), proj.reshape(-1), table.T
    qkv, proj, table = local_grads(False, norm, *args, None)
    qkv_mine = lax.psum_scatter(qkv.reshape(-1), AXES, tiled=True)
    proj_mine = lax.psum_scatter(proj.reshape(-1), AXES, tiled=True)
    table = lax.psum(table, AXES)
    return (
        0.9 * mom_qkv + qkv_mine * norm,
        0.9 * mom_proj + proj_mine * norm,
        0.9 * mom_table + table.T * norm,
    )


def solution(mesh):
    return jax.shard_map(
        body,
        mesh=mesh,
        in_specs=(
            P(AXES, None, None),
            P(AXES, None, None),
            P(AXES, None),
            P(),
            P(),
            P(),
            P(),
            P(AXES),
            P(AXES),
            P(),
        ),
        out_specs=(P(AXES), P(AXES), P()),
        check_vma=False,
    )
```

time: 116 us -> 59 us (0.51)
  Pallas kernels: 105 us -> 53.9 us
  other arithmetic: 4.27 us -> 0 us
  local copies, waits for them, and re-layouts: 5.48 us -> 4.24 us
    pallas_call x1, Pallas kernels: 105 us -> 53.9 us  [local_grads(): pl.pallas_call(functools.partial(kernel, dims, [*inputs, *outs, *scratch]...]
    add x3 -> x0, other arithmetic: 2.61 us -> none  [the longest x1 1.33 us: body(): 0.9 * mom_table + table[:, :entries].T * scale]
    unnamed x12 -> x3, local copies, waits for them, and re-layouts: 5.47 us -> 4.24 us
where the time goes in v1:
time: 59 us; the launch traced here: 58.7 us
  Pallas kernels  53.9 us (91%)
  local copies, waits for them, and re-layouts  4.24 us (7%)
  between operations  0.64 us (1%)
    pallas_call x1, Pallas kernels, local_grads(): pl.pallas_call(functools.partial(kernel, dims, [*inputs, *outs, *scratch]...  53.9 us
    unnamed x3, local copies, waits for them, and re-layouts  4.24 us

profile of v1, /device:TPU:0, one launch (start us, length us, event | category | flops | bytes accessed | tf_op | source)
XLA Modules:
  0.0 58.7 jit_solution(1405672767501268909)
XLA Ops:
  0.6 53.9 %shard_map.121 = (f32[192,128]{1,0:T(8,128)}, f32[64,128]{1,0:T(8,128)}, f32[16,169]{1,0:T(8,128)}) custom-call(bf16[49,16,512]{2,1,0:T(8,128)(2,1)} %bitcast.9, bf16[49,16,512]{2,1,0:T(8,128)(2,1)} %bitcast.10, s32[16,49]{1,0:T(8,128)} %all_refs_2_.1, s32[49,49]{1,0:T(8,128)} %all_refs_3_.1, bf16[512,1536]{1,0:T(8,128)(2,1)} %all_refs_4_.1, ...), custom_call_target="tpu_custom_call" | custom-call | tf_op jit(solution)/shard_map/pallas_call | solution.py:510
  54.5 1.5 %copy.16 = f32[24576]{0:T(1024)} copy(f32[24576]{0:T(1024)} %bitcast.11) | data formatting | bytes 196608
  56.0 1.4 %copy.17 = f32[8192]{0:T(1024)} copy(f32[8192]{0:T(1024)} %bitcast.14) | data formatting | bytes 65536
  57.4 1.3 %copy.18 = f32[169,16]{0,1:T(8,128)} copy(f32[169,16]{0,1:T(8,128)} %bitcast.17) | data formatting | bytes 21632

commit v2 on v1

--- a/solution.py
+++ b/solution.py
@@ -13,11 +13,24 @@
 F32, BF16 = jnp.float32, jnp.bfloat16
 PAD = 64
 GROUP = 4
+BATCH = 4
 LOG2E = math.log2(math.e)
 NT = (((1,), (1,)), ((), ()))
 TN = (((0,), (0,)), ((), ()))
 COPIES = 8
-DUE = (3, 6, 5, 7)
+SPEED = (680e3, 98e3, 98e3, 98e3)
+DELAY = (1.4, 3.0, 2.6, 4.0)
+
+
+class Clock:
+    def __init__(self):
+        self.now, self.free = 0.0, dict(core=0.0, xy=0.0, z=0.0)
+
+    def arrival(self, stage, size):
+        link = ("core", "xy", "xy", "z")[stage]
+        done = max(self.now, self.free[link]) + size / SPEED[stage]
+        self.free[link] = done
+        return done + DELAY[stage]
 
 
 def dot(a, b, dims=(((1,), (0,)), ((), ()))):
@@ -54,13 +67,15 @@
 
 
 class Chunk:
-    def __init__(self, place, refs, send, recv, due, finish):
-        self.p = place
+    def __init__(self, place, refs, send, recv, clock, finish):
+        self.p, self.clock = place, clock
         self.buf, self.r0, self.r1, self.r2, self.s2, self.r3 = refs
         self.send, self.recv, self.finish = send, recv, finish
         self.ab = ((place.x, place.y), (place.y, place.x))
         self.via = ((place.to_x, place.to_y), (place.to_y, place.to_x))
-        self.stage, self.due = 0, due
+        self.stage, self.due = 0, None
+        whole = 4 * math.prod(self.buf.shape)
+        self.sizes = (whole / 2, whole / 4, whole / 8, whole / 4)
 
     def copy(self, n, src, dst, there):
         return pltpu.make_async_remote_copy(
@@ -96,6 +111,7 @@
     def start(self):
         for c in self.copies(0):
             c.start()
+        self.due = self.clock.arrival(0, self.sizes[0])
 
     def advance(self):
         p, buf, stage = self.p, self.buf, self.stage
@@ -129,14 +145,16 @@
                 c.wait()
             self.finish(self.s2[p.z] + self.r3[0] + self.r3[1] + self.r3[2])
         self.stage += 1
+        if self.stage < 4:
+            self.due = self.clock.arrival(self.stage, self.sizes[self.stage])
 
 
 class Table:
-    def __init__(self, place, refs, send, recv, due, finish):
-        self.p = place
+    def __init__(self, place, refs, send, recv, clock, finish):
+        self.p, self.clock = place, clock
         self.t0, self.r0, self.t1, self.r1, self.r2 = refs
         self.send, self.recv, self.finish = send, recv, finish
-        self.stage, self.due = 1, due
+        self.stage, self.due, self.size = 1, None, 4 * math.prod(self.t0.shape)
 
     def copy(self, n, src, dst, there):
         return pltpu.make_async_remote_copy(
@@ -162,6 +180,7 @@
     def start(self):
         for c in self.copies(1):
             c.start()
+        self.due = self.clock.now + 1.5
 
     def advance(self):
         for c in self.copies(self.stage):
@@ -181,28 +200,27 @@
         if self.stage < 3:
             for c in self.copies(self.stage + 1):
                 c.start()
+            self.due = self.clock.arrival(self.stage, 4 * self.size) + 0.5
         self.stage += 1
 
 
 def kernel(dims, names, *all_refs):
-    win, count, dim, heads, entries, remote, norm = dims
+    win, count, dim, heads, entries, remote = dims
     r = dict(zip(names, all_refs, strict=True))
     width = dim // heads
     groups = heads // GROUP
     wide = GROUP * width
     scale = width**-0.5
-    x, xt, c, qkv, d_att, att = r["x"], r["xt"], r["c"], r["qkv"], r["d_att"], r["att"]
+    x, xt, c, qkv, d_att, att_t = r["x"], r["xt"], r["c"], r["qkv"], r["d_att"], r["att_t"]
     d_v, d_qk, probs, masks = r["d_v"], r["d_qk"], r["probs"], r["masks"]
     bias, bias_rows, d_bias, small, rel_t, tab = (
         r[n] for n in ("bias", "bias_rows", "d_bias", "small", "rel_t", "tab")
     )
-    fetched = [("tok", "tok_v"), ("w_qkv", "w_qkv_v"), ("cot", "cot_v"), ("w_proj", "w_proj_v")]
-    fetch = [
-        pltpu.make_async_copy(r[a], r[b], r["fetch"].at[n]) for n, (a, b) in enumerate(fetched)
-    ]
-    for f in fetch:
-        f.start()
-    w_qkv, w_proj = r["w_qkv_v"], r["w_proj_v"]
+    fetch = {}
+    for n, name in enumerate(n[:-3] for n in names if n.endswith("_vm")):
+        fetch[name] = pltpu.make_async_copy(r[name], r[f"{name}_vm"], r["fetch"].at[n])
+        fetch[name].start()
+    w_qkv, w_proj = r["w_qkv_vm"], r["w_proj_vm"]
 
     if remote:
         place = Place()
@@ -212,8 +230,10 @@
 
     lanes = lax.broadcasted_iota(jnp.int32, (PAD, wide), 1)
 
+    for name in ("reg", "rel", "table"):
+        fetch[name].wait()
     small[...] = jnp.zeros_like(small)
-    small[0:win, 0:count] = r["reg"][...].astype(F32)
+    small[0:win, 0:count] = r["reg_vm"][...].astype(F32)
     reg_rows = small[...]
     reg_cols = reg_rows.T
     for w in range(win):
@@ -224,10 +244,10 @@
         )
 
     small[...] = jnp.full_like(small, -1.0)
-    small[0:count, 0:count] = r["rel"][...].astype(F32)
+    small[0:count, 0:count] = r["rel_vm"][...].astype(F32)
     rel_t[...] = small[...].T
     tab[...] = jnp.zeros_like(tab)
-    tab[:, 0:entries] = r["table"][...]
+    tab[:, 0:entries] = r["table_vm"][...]
     size = tab.shape[1]
     tab_t = tab[...]
     high = tab_t.astype(BF16)
@@ -271,19 +291,26 @@
             for w in range(win):
                 dst[w * PAD : (w + 1) * PAD, cols] = flat[n, pl.ds(w, PAD, stride=win), :].astype(BF16)
 
-    fetch[0].wait()
-    by_window(r["tok_v"], x)
-    fetch[2].wait()
-    by_window(r["cot_v"], c)
-    fetch[1].wait()
-    fetch[3].wait()
-
-    @pl.loop(0, rows_all // 256)
-    def _(i):
-        rows = pl.ds(pl.multiple_of(i * 256, 256), 256)
-        qkv[rows, :] = dot(x[rows, :], w_qkv[...]).astype(BF16)
-        d_att[rows, :] = dot(c[rows, :], w_proj[...], NT).astype(BF16)
-
+    fetch["tok"].wait()
+    by_window(r["tok_vm"], x)
+    fetch["cot"].wait()
+    by_window(r["cot_vm"], c)
+    fetch["w_qkv"].wait()
+    fetch["w_proj"].wait()
+
+    def project(n):
+        half = dim // 2
+
+        @pl.loop(0, rows_all // 256)
+        def _(i):
+            rows = pl.ds(pl.multiple_of(i * 256, 256), 256)
+            for which in range(3):
+                cols = slice(which * dim + n * half, which * dim + (n + 1) * half)
+                qkv[rows, cols] = dot(x[rows, :], w_qkv[:, cols]).astype(BF16)
+            cols = slice(n * half, (n + 1) * half)
+            d_att[rows, cols] = dot(c[rows, :], w_proj[cols, :], NT).astype(BF16)
+
+    project(0)
     xt[...] = x[...].T
 
     def rows_of(w):
@@ -294,28 +321,42 @@
         at = which * dim + g * wide
         return ref[rows, at : at + wide]
 
-    def forward(w, carry):
-        rows = rows_of(w)
-        mask = masks[rows, :]
-        mask = jnp.concatenate([mask] * (GROUP * PAD // 128), axis=1)
-        every = range(groups)
-        queries = [spread(part(qkv, 0, g, rows), lanes, width) for g in every]
-        d_out = [spread(part(d_att, 0, g, rows), lanes, width) for g in every]
-        scores = [dot(part(qkv, 1, g, rows), queries[g], NT) for g in every]
-        scores = [scores[g] * (scale * LOG2E) + bias[g] + mask for g in every]
-        raised = [jnp.exp2(v - jnp.max(v, axis=0, keepdims=True)) for v in scores]
-        p = [(v * (1.0 / jnp.sum(v, axis=0, keepdims=True))).astype(BF16) for v in raised]
-        mixed = [dot(p[g], part(qkv, 2, g, rows), TN) for g in every]
-        d_v[rows, :] = jnp.concatenate([dot(p[g], d_out[g]) for g in every], axis=1).astype(BF16)
-        joined = [gather_heads(v, lanes, width).astype(BF16) for v in mixed]
-        att[rows, :] = jnp.concatenate(joined, axis=1)
-        for g in every:
-            probs[g, rows, :] = p[g]
-        return carry
-
-    lax.fori_loop(0, win, forward, 0)
-
-    tick = 0
+    ring, ring_ds = r["ring"], r["ring_ds"]
+
+    def pipelined(batches, stages, after):
+        for s in range(len(batches) + len(stages) - 1):
+            for k in reversed(range(len(stages))):
+                if 0 <= s - k < len(batches):
+                    stages[k](batches[s - k], (s - k) % 2 * BATCH)
+            after(s - len(stages) + 1)
+
+    def get_scores(units, at):
+        for n, (g, w) in enumerate(units):
+            rows = rows_of(w)
+            query = spread(part(qkv, 0, g, rows), lanes, width)
+            ring[at + n] = dot(part(qkv, 1, g, rows), query, NT)
+
+    def get_probs(units, at):
+        for n, (g, w) in enumerate(units):
+            rows = rows_of(w)
+            mask = jnp.concatenate([masks[rows, :]] * (GROUP * PAD // 128), axis=1)
+            v = ring[at + n] * (scale * LOG2E) + bias[g] + mask
+            v = jnp.exp2(v - jnp.max(v, axis=0, keepdims=True))
+            probs[g, rows, :] = (v * (1.0 / jnp.sum(v, axis=0, keepdims=True))).astype(BF16)
+
+    def use_probs(units, at):
+        for g, w in units:
+            rows = rows_of(w)
+            p = probs[g, rows, :]
+            mixed = dot(part(qkv, 2, g, rows), p, TN).astype(BF16)
+            for h in range(GROUP):
+                att_t[g * wide + h * width : g * wide + (h + 1) * width, rows] = mixed[
+                    h * width : (h + 1) * width, h * PAD : (h + 1) * PAD
+                ]
+            d_out = spread(part(d_att, 0, g, rows), lanes, width)
+            d_v[rows, g * wide : (g + 1) * wide] = dot(p, d_out).astype(BF16)
+
+    clock = Clock()
     active = []
 
     def put(value, ref):
@@ -325,81 +366,113 @@
                 a, b = (dx, dy) if half == 0 else (dy, dx)
                 ref[dc, half, a, b, dz] = value[16 * d + 8 * half : 16 * d + 8 * half + 8]
 
-    def update(out, mom, at, tiles, value):
+    def update(out, at, tiles, value):
         for half in range(2):
             for n in range(value.shape[2] // 128):
                 rows = pl.ds(half * 8 * tiles + at(n), 8, stride=tiles)
-                out[rows, :] = 0.9 * mom[rows, :] + value[half, :, n * 128 : n * 128 + 128] * norm
+                out[rows, :] = value[half, :, n * 128 : n * 128 + 128]
 
     def ship(name, n, value, finish):
         refs = [r[f"{name}_{k}"] for k in ("buf", "r0", "r1", "r2", "s2", "r3")]
         put(value, refs[0])
-        chunk = Chunk(place, refs, r["send"].at[n], r["recv"].at[n], tick + DUE[0], finish)
+        chunk = Chunk(place, refs, r["send"].at[n], r["recv"].at[n], clock, finish)
         chunk.start()
         active.append(chunk)
 
-    def run_due(limit):
+    def run_due(passed, last=False):
+        clock.now += passed
         while True:
-            ready = [k for k in active if k.stage < 4 and k.due <= limit]
+            ready = [k for k in active if k.stage < 4 and (last or k.stage < 3 and k.due <= clock.now)]
             if not ready:
                 return
-            first = min(ready, key=lambda k: k.due)
+            first = min(ready, key=lambda k: (k.stage == 3, k.due))
+            clock.now = max(clock.now, first.due)
             first.advance()
-            if first.stage < 4:
-                first.due += DUE[first.stage]
 
     if remote:
         pl.semaphore_wait(barrier, len(place.everyone()))
     tiles = dim // 128
-    g_v = dot(xt[...], d_v[...])
-    if remote:
-        ship("v", 0, g_v, functools.partial(update, r["out_qkv"], r["mom_qkv"], lambda n: 2 * tiles + n, 3 * tiles))
-    else:
-        r["out_qkv"][:, 2 * dim :] = g_v
-    g_proj = dot(att[...], c[...], TN)
-    tick += 2
-    if remote:
-        ship("p", 1, g_proj, functools.partial(update, r["out_proj"], r["mom_proj"], lambda n: n, tiles))
-    else:
-        r["out_proj"][...] = g_proj
-
-    def backward(g, windows):
-        rows = [rows_of(w) for w in windows]
-        queries = [spread(part(qkv, 0, g, rw), lanes, width) for rw in rows]
-        d_out = [spread(part(d_att, 0, g, rw), lanes, width) for rw in rows]
-        p = [probs[g, rw, :] for rw in rows]
-        every = range(len(rows))
-        d_probs = [dot(part(qkv, 2, g, rows[n]), d_out[n], NT) for n in every]
-        pf = [v.astype(F32) for v in p]
-        weighted = [pf[n] * d_probs[n] for n in every]
-        d_scores = [
-            weighted[n] - pf[n] * jnp.sum(weighted[n], axis=0, keepdims=True) for n in every
-        ]
-        d_bias[g] += sum(d_scores[1:], d_scores[0])
-        ds = [v.astype(BF16) for v in d_scores]
-        d_k = [dot(ds[n], queries[n]) * scale for n in every]
-        d_q = [dot(ds[n], part(qkv, 1, g, rows[n]), TN) for n in every]
-        d_q = [gather_heads(v, lanes, width) * scale for v in d_q]
-        for n in every:
-            d_qk[rows[n], :] = jnp.concatenate([d_q[n], d_k[n]], axis=1).astype(BF16)
-
-    pieces = 4
-    for g in range(groups):
-        for s in range(pieces):
-            backward(g, range(s * win // pieces, (s + 1) * win // pieces))
-            tick += 1
+    per = wide // 128
+    half = dim // 2
+    pairs = groups // 2
+    for n in range(pairs):
+        units = [(g, w) for w in range(win) for g in (2 * n, 2 * n + 1)]
+        batches = [units[k : k + BATCH] for k in range(0, len(units), BATCH)]
+
+        def after(done):
+            if remote and done % 2 == 1:
+                run_due(0.45)
+
+        if n:
+            project(n)
             if remote:
-                run_due(tick)
-        g_qk = dot(xt[...], d_qk[...])
-        tick += 1
-        per = wide // 128
+                run_due(1.4)
+        pipelined(batches, (get_scores, get_probs, use_probs), after)
+        cols = slice(2 * n * wide, 2 * (n + 1) * wide)
+        g_v = dot(xt[...], d_v[:, cols])
+        if remote:
+            at = lambda k, n=n: 2 * tiles + 2 * n * per + k
+            ship(f"v{n}", n, g_v, functools.partial(update, r["out_qkv"], at, 3 * tiles))
+            run_due(0.5)
+        else:
+            r["out_qkv"][:, 2 * dim + cols.start : 2 * dim + cols.stop] = g_v
+    for n in range(2):
+        cols = slice(n * half, (n + 1) * half)
+        g_proj = dot(att_t[...], c[:, cols])
+        if remote:
+            at = lambda k, n=n: n * tiles // 2 + k
+            ship(f"p{n}", pairs + n, g_proj, functools.partial(update, r["out_proj"], at, tiles))
+            run_due(0.6)
+        else:
+            r["out_proj"][:, cols] = g_proj
+
+    def get_d_probs(units, at):
+        for n, (g, w) in enumerate(units):
+            rows = rows_of(w)
+            d_out = spread(part(d_att, 0, g, rows), lanes, width)
+            ring[at + n] = dot(part(qkv, 2, g, rows), d_out, NT)
+
+    def get_d_scores(units, at):
+        g = units[0][0]
+        total = d_bias[g]
+        for n, (_, w) in enumerate(units):
+            pf = probs[g, rows_of(w), :].astype(F32)
+            weighted = pf * ring[at + n]
+            ds = weighted - pf * jnp.sum(weighted, axis=0, keepdims=True)
+            total = total + ds
+            ring_ds[at + n] = ds.astype(BF16)
+        d_bias[g] = total
+
+    def use_d_scores(units, at):
+        for n, (g, w) in enumerate(units):
+            rows = rows_of(w)
+            ds = ring_ds[at + n]
+            d_k = dot(ds, spread(part(qkv, 0, g, rows), lanes, width)) * scale
+            d_q = gather_heads(dot(ds, part(qkv, 1, g, rows), TN), lanes, width) * scale
+            d_qk[g % 2, rows, :] = jnp.concatenate([d_q, d_k], axis=1).astype(BF16)
+
+    def send_qk(g):
+        g_qk = dot(xt[...], d_qk[g % 2])
         if remote:
             at = lambda n, g=g: (n // per) * tiles + g * per + n % per
-            ship(f"k{g}", 2 + g, g_qk, functools.partial(update, r["out_qkv"], r["mom_qkv"], at, 3 * tiles))
+            ship(f"k{g}", pairs + 2 + g, g_qk, functools.partial(update, r["out_qkv"], at, 3 * tiles))
+            run_due(0.5)
         else:
             for which in range(2):
                 at = which * dim + g * wide
                 r["out_qkv"][:, at : at + wide] = g_qk[:, which * wide : (which + 1) * wide]
+
+
+    units = [(g, w) for g in range(groups) for w in range(win)]
+    batches = [units[k : k + BATCH] for k in range(0, len(units), BATCH)]
+
+    def after_backward(done):
+        if remote and done % 2 == 0:
+            run_due(0.6)
+        if done >= 0 and (done + 1) * BATCH % win == 0:
+            send_qk(batches[done][0][0])
+
+    pipelined(batches, (get_d_probs, get_d_scores, use_d_scores), after_backward)
 
     for g in range(groups):
         for h in range(GROUP):
@@ -418,27 +491,31 @@
         return total
 
     if remote:
-        tick += 1
-        run_due(tick)
-    g_table = lax.fori_loop(0, count // unroll, collect, jnp.zeros((2 * heads, size), F32))
+        run_due(0.3)
+    g_table = jnp.zeros((2 * heads, size), F32)
+    steps = count // unroll
+    for k in range(2):
+        g_table = lax.fori_loop(k * steps // 2, (k + 1) * steps // 2, collect, g_table)
+        if remote:
+            run_due(0.9)
     g_table = g_table[:heads] + g_table[heads:]
     if not remote:
         r["out_table"][...] = g_table[:, :entries]
         return
-    tick += 2
     refs = [r[f"t_{k}"] for k in ("t0", "r0", "t1", "r1", "r2")]
     refs[0][...] = g_table
 
     def table_done(value):
-        r["out_table"][...] = 0.9 * r["mom_table"][...] + value[:, :entries] * norm
-
-    last = Table(place, refs, r["send"].at[2 + groups], r["recv"].at[2 + groups], tick + 2, table_done)
+        r["out_table"][...] = value[:, :entries]
+
+    n = pairs + 2 + groups
+    last = Table(place, refs, r["send"].at[n], r["recv"].at[n], clock, table_done)
     last.start()
     active.append(last)
-    run_due(10**6)
-
-
-def local_grads(remote, norm, tokens, cotangent, regions, rel_index, w_qkv, w_proj, bias_table, moms):
+    run_due(0.0, True)
+
+
+def local_grads(remote, tokens, cotangent, regions, rel_index, w_qkv, w_proj, bias_table):
     win, count, dim = tokens.shape
     entries, heads = bias_table.shape
     groups = heads // GROUP
@@ -447,39 +524,35 @@
     size = -(-entries // 128) * 128
     own = dim // 32
     inputs = dict(
-        tok=tokens.transpose(1, 0, 2),
-        cot=cotangent.transpose(1, 0, 2),
         reg=regions,
         rel=rel_index,
+        table=bias_table.T,
+        tok=tokens.transpose(1, 0, 2),
         w_qkv=w_qkv,
+        cot=cotangent.transpose(1, 0, 2),
         w_proj=w_proj,
-        table=bias_table.T,
     )
     if remote:
-        inputs |= dict(
-            mom_qkv=moms[0].reshape(-1, 128), mom_proj=moms[1].reshape(-1, 128), mom_table=moms[2].T
-        )
         outs = dict(
             out_qkv=(own * 3 * dim // 128, 128), out_proj=(own * dim // 128, 128), out_table=(heads, entries)
         )
     else:
         outs = dict(out_qkv=(dim, 3 * dim), out_proj=(dim, dim), out_table=(heads, entries))
     vmem = pltpu.VMEM
-    scratch = dict(
-        fetch=pltpu.SemaphoreType.DMA((4,)),
-        tok_v=vmem((count, win, dim), BF16),
-        cot_v=vmem((count, win, dim), BF16),
-        w_qkv_v=vmem((dim, 3 * dim), BF16),
-        w_proj_v=vmem((dim, dim), BF16),
+    scratch = {f"{n}_vm": vmem(v.shape, v.dtype) for n, v in inputs.items()}
+    scratch |= dict(
+        fetch=pltpu.SemaphoreType.DMA((len(inputs),)),
         flat=vmem((dim // 128, rows, 128), F32),
         x=vmem((rows, dim), BF16),
         xt=vmem((dim, rows), BF16),
         c=vmem((rows, dim), BF16),
         qkv=vmem((rows, 3 * dim), BF16),
         d_att=vmem((rows, dim), BF16),
-        att=vmem((rows, dim), BF16),
+        att_t=vmem((dim, rows), BF16),
         d_v=vmem((rows, dim), BF16),
-        d_qk=vmem((rows, 2 * wide), BF16),
+        d_qk=vmem((2, rows, 2 * wide), BF16),
+        ring=vmem((2 * BATCH, PAD, GROUP * PAD), F32),
+        ring_ds=vmem((2 * BATCH, PAD, GROUP * PAD), BF16),
         probs=vmem((groups, rows, GROUP * PAD), BF16),
         masks=vmem((rows, 128), F32),
         bias=vmem((groups, PAD, GROUP * PAD), F32),
@@ -491,7 +564,8 @@
     )
     params = dict()
     if remote:
-        chunks = dict(v=dim, p=dim) | {f"k{g}": 2 * wide for g in range(groups)}
+        chunks = {f"v{n}": 2 * wide for n in range(groups // 2)} | dict(p0=dim // 2, p1=dim // 2)
+        chunks |= {f"k{g}": 2 * wide for g in range(groups)}
         for name, cols in chunks.items():
             scratch[f"{name}_buf"] = vmem((2, 2, 2, 2, 4, 8, cols), F32)
             scratch[f"{name}_r0"] = vmem((2, 2, 2, 4, 8, cols), F32)
@@ -504,17 +578,32 @@
         scratch["send"] = pltpu.SemaphoreType.DMA((len(chunks) + 1, COPIES))
         scratch["recv"] = pltpu.SemaphoreType.DMA((len(chunks) + 1, COPIES))
         params = dict(collective_id=0, has_side_effects=True)
-    dims = (win, count, dim, heads, entries, remote, norm)
+    dims = (win, count, dim, heads, entries, remote)
     spec = pl.BlockSpec(memory_space=pltpu.VMEM)
-    where = {n: pl.BlockSpec(memory_space=pl.ANY) for n in ("tok", "cot", "w_qkv", "w_proj")}
     return pl.pallas_call(
         functools.partial(kernel, dims, [*inputs, *outs, *scratch]),
         out_shape=[jax.ShapeDtypeStruct(o, F32) for o in outs.values()],
-        in_specs=[where.get(n, spec) for n in inputs],
+        in_specs=[pl.BlockSpec(memory_space=pl.ANY)] * len(inputs),
         out_specs=[spec] * len(outs),
         scratch_shapes=list(scratch.values()),
         compiler_params=pltpu.CompilerParams(vmem_limit_bytes=60 * 1024 * 1024, **params),
     )(*inputs.values())
+
+
+def momentum_kernel(norm, *refs):
+    for grad, old, new in zip(refs[:3], refs[3:6], refs[6:], strict=True):
+        new[...] = 0.9 * old[...] + grad[...] * norm
+
+
+def momentum(norm, grads, moms):
+    old = [m.reshape(g.shape) if m.ndim == 1 else m.T for g, m in zip(grads, moms, strict=True)]
+    spec = pl.BlockSpec(memory_space=pltpu.VMEM)
+    return pl.pallas_call(
+        functools.partial(momentum_kernel, norm),
+        out_shape=[jax.ShapeDtypeStruct(g.shape, F32) for g in grads],
+        in_specs=[spec] * 6,
+        out_specs=[spec] * 3,
+    )(*grads, *old)
 
 
 def body(
@@ -525,11 +614,11 @@
     sizes = tuple(lax.axis_size(a) for a in AXES)
     norm = 1.0 / (tokens.shape[0] * devices)
     args = (tokens, cotangent, regions, rel_index, w_qkv, w_proj, bias_table)
-    moms = (mom_qkv, mom_proj, mom_table)
     if sizes == (2, 4, 4) and dim == 16 * devices:
-        qkv, proj, table = local_grads(True, norm, *args, moms)
+        grads = local_grads(True, *args)
+        qkv, proj, table = momentum(norm, grads, (mom_qkv, mom_proj, mom_table))
         return qkv.reshape(-1), proj.reshape(-1), table.T
-    qkv, proj, table = local_grads(False, norm, *args, None)
+    qkv, proj, table = local_grads(False, *args)
     qkv_mine = lax.psum_scatter(qkv.reshape(-1), AXES, tiled=True)
     proj_mine = lax.psum_scatter(proj.reshape(-1), AXES, tiled=True)
     table = lax.psum(table, AXES)

time: 59 us -> 47 us (0.80)
  Pallas kernels: 53.9 us -> 46.1 us
  local copies, waits for them, and re-layouts: 4.24 us -> 0 us
    pallas_call x1, Pallas kernels: 53.9 us -> 44.5 us  [local_grads(): pl.pallas_call(functools.partial(kernel, dims, [*inputs, *outs, *scratch]...]
    unnamed x3 -> x0, local copies, waits for them, and re-layouts: 4.24 us -> none
    pallas_call x0 -> x1, Pallas kernels: none -> 1.63 us  [momentum(): pl.pallas_call(functools.partial(momentum_kernel, norm), out_shape=[jax.S...]
where the time goes in v2:
time: 47 us; the launch traced here: 46.7 us
  Pallas kernels  46.1 us (98%)
  between operations  0.64 us (1%)
    pallas_call x1, Pallas kernels, local_grads(): pl.pallas_call(functools.partial(kernel, dims, [*inputs, *outs, *scratch]...  44.5 us
    pallas_call x1, Pallas kernels, momentum(): pl.pallas_call(functools.partial(momentum_kernel, norm), out_shape=[jax.S...  1.63 us

profile of v2, /device:TPU:0, one launch (start us, length us, event | category | flops | bytes accessed | tf_op | source)
XLA Modules:
  0.0 46.7 jit_solution(6102138497282413029)
XLA Ops:
  0.6 44.5 %shard_map.121 = (f32[192,128]{1,0:T(8,128)}, f32[64,128]{1,0:T(8,128)}, f32[16,169]{1,0:T(8,128)}) custom-call(s32[16,49]{1,0:T(8,128)} %all_refs_0_.1, s32[49,49]{1,0:T(8,128)} %all_refs_1_.1, f32[16,169]{1,0:T(8,128)} %bitcast.13, bf16[49,16,512]{2,1,0:T(8,128)(2,1)} %bitcast.9, bf16[512,1536]{1,0:T(8,128)(2,1)} %all_refs_4_.1, ...), custom_call_target="tpu_custom_call" | custom-call | tf_op jit(solution)/shard_map/pallas_call | solution.py:583
  45.1 1.6 %shard_map.122 = (f32[192,128]{1,0:T(8,128)}, f32[64,128]{1,0:T(8,128)}, f32[16,169]{1,0:T(8,128)}) custom-call(f32[192,128]{1,0:T(8,128)} %get-tuple-element.9.refs_0_, f32[64,128]{1,0:T(8,128)} %get-tuple-element.10.refs_1_, f32[16,169]{1,0:T(8,128)} %get-tuple-element.11.refs_2_, f32[192,128]{1,0:T(8,128)} %bitcast.11, f32[64,128]{1,0:T(8,128)} %bitcast.12, ...), custom_call_target="tpu_custom_call" | custom-call | tf_op jit(solution)/shard_map/pallas_call | solution.py:601

commit v3 on v2

--- a/solution.py
+++ b/solution.py
@@ -14,23 +14,28 @@
 PAD = 64
 GROUP = 4
 BATCH = 4
+MSPLIT = 2
 LOG2E = math.log2(math.e)
 NT = (((1,), (1,)), ((), ()))
 TN = (((0,), (0,)), ((), ()))
 COPIES = 8
-SPEED = (680e3, 98e3, 98e3, 98e3)
-DELAY = (1.4, 3.0, 2.6, 4.0)
+SPEED = dict(core=680e3, xy=98e3, z=98e3)
+DELAY = dict(core=1.4, xy=2.4, z=4.0)
+
+
+def tall_dot(a, b):
+    step = a.shape[0] // MSPLIT
+    return jnp.concatenate([dot(a[k * step : (k + 1) * step, :], b) for k in range(MSPLIT)], axis=0)
 
 
 class Clock:
     def __init__(self):
         self.now, self.free = 0.0, dict(core=0.0, xy=0.0, z=0.0)
 
-    def arrival(self, stage, size):
-        link = ("core", "xy", "xy", "z")[stage]
-        done = max(self.now, self.free[link]) + size / SPEED[stage]
+    def arrival(self, link, size):
+        done = max(self.now, self.free[link]) + size / SPEED[link]
         self.free[link] = done
-        return done + DELAY[stage]
+        return done + DELAY[link]
 
 
 def dot(a, b, dims=(((1,), (0,)), ((), ()))):
@@ -67,6 +72,11 @@
 
 
 class Chunk:
+    links = ("core", "xy", "xy", "z")
+
+    def set_sizes(self, whole):
+        self.sizes = (whole / 2, whole / 4, whole / 8, whole / 4)
+
     def __init__(self, place, refs, send, recv, clock, finish):
         self.p, self.clock = place, clock
         self.buf, self.r0, self.r1, self.r2, self.s2, self.r3 = refs
@@ -74,8 +84,7 @@
         self.ab = ((place.x, place.y), (place.y, place.x))
         self.via = ((place.to_x, place.to_y), (place.to_y, place.to_x))
         self.stage, self.due = 0, None
-        whole = 4 * math.prod(self.buf.shape)
-        self.sizes = (whole / 2, whole / 4, whole / 8, whole / 4)
+        self.set_sizes(4 * math.prod(self.buf.shape))
 
     def copy(self, n, src, dst, there):
         return pltpu.make_async_remote_copy(
@@ -108,10 +117,13 @@
             ]
         return [self.copy(5 + k, self.s2.at[p.others[k]], self.r3.at[k], p.to_z[k]) for k in range(3)]
 
+    def final(self):
+        return self.stage == 3
+
     def start(self):
         for c in self.copies(0):
             c.start()
-        self.due = self.clock.arrival(0, self.sizes[0])
+        self.due = self.clock.arrival("core", self.sizes[0])
 
     def advance(self):
         p, buf, stage = self.p, self.buf, self.stage
@@ -143,18 +155,70 @@
         else:
             for c in waited:
                 c.wait()
-            self.finish(self.s2[p.z] + self.r3[0] + self.r3[1] + self.r3[2])
+            done = self.s2[p.z] + self.r3[0] + self.r3[1] + self.r3[2]
+            self.finish([done[0], done[1]])
         self.stage += 1
         if self.stage < 4:
-            self.due = self.clock.arrival(self.stage, self.sizes[self.stage])
+            self.due = self.clock.arrival(self.links[self.stage], self.sizes[self.stage])
+
+
+class ChunkZ(Chunk):
+    links = ("core", "z", "xy", "xy")
+
+    def set_sizes(self, whole):
+        self.sizes = (whole / 2, whole, whole / 16, whole / 32)
+
+    def copies(self, stage):
+        p, buf = self.p, self.buf
+        if stage == 0:
+            return [self.copy(0, buf.at[1 - p.core], self.r0, p.to_core)]
+        if stage == 1:
+            return [self.copy(1 + k, buf.at[p.core, p.others[k]], self.r1.at[k], p.to_z[k]) for k in range(3)]
+        if stage == 2:
+            return [
+                self.copy(4 + h, self.s2.at[h, 1 - self.ab[h][0]], self.r2.at[h], self.via[h][0])
+                for h in range(2)
+            ]
+        return [
+            self.copy(6 + h, self.s2.at[h, self.ab[h][0], 1 - self.ab[h][1]], self.r3.at[h], self.via[h][1])
+            for h in range(2)
+        ]
+
+    def advance(self):
+        p, buf, s2, stage = self.p, self.buf, self.s2, self.stage
+        waited = self.copies(stage)
+        after = self.copies(stage + 1) if stage < 3 else []
+        for c in waited:
+            c.wait()
+        if stage == 0:
+            for k, z in enumerate(p.others):
+                buf[p.core, z] = buf[p.core, z] + self.r0[z]
+                after[k].start()
+        elif stage == 1:
+            for h in range(2):
+                for a in (1 - self.ab[h][0], self.ab[h][0]):
+                    s2[h, a] = (buf[p.core, p.z, h, a] + self.r0[p.z, h, a]) + (
+                        self.r1[0, h, a] + self.r1[1, h, a] + self.r1[2, h, a]
+                    )
+                after[h].start()
+        elif stage == 2:
+            for h in range(2):
+                a = self.ab[h][0]
+                s2[h, a] = s2[h, a] + self.r2[h]
+                after[h].start()
+        else:
+            self.finish([s2[h, self.ab[h][0], self.ab[h][1]] + self.r3[h] for h in range(2)])
+        self.stage += 1
+        if self.stage < 4:
+            self.due = self.clock.arrival(self.links[self.stage], self.sizes[self.stage])
 
 
 class Table:
     def __init__(self, place, refs, send, recv, clock, finish):
         self.p, self.clock = place, clock
-        self.t0, self.r0, self.t1, self.r1, self.r2 = refs
+        self.t0, self.r0, self.t1, self.r1, self.r2, self.t3 = refs
         self.send, self.recv, self.finish = send, recv, finish
-        self.stage, self.due, self.size = 1, None, 4 * math.prod(self.t0.shape)
+        self.stage, self.due, self.size = 0, None, 4 * math.prod(self.t1.shape)
 
     def copy(self, n, src, dst, there):
         return pltpu.make_async_remote_copy(
@@ -168,40 +232,52 @@
 
     def copies(self, stage):
         p = self.p
+        if stage == 0:
+            return [self.copy(0, self.t0.at[1 - p.core], self.r0, p.to_core)]
         if stage == 1:
-            return [self.copy(0, self.t0, self.r0, p.to_core)]
-        if stage == 2:
             return [
                 self.copy(1 + k, self.t1, self.r1.at[k], there)
                 for k, there in enumerate((p.to_x, p.to_y, p.to_xy))
             ]
-        return [self.copy(4 + k, self.r2.at[p.z], self.r2.at[p.z], p.to_z[k]) for k in range(3)]
+        if stage == 2:
+            return [self.copy(4 + k, self.r2.at[p.z], self.r2.at[p.z], p.to_z[k]) for k in range(3)]
+        return [self.copy(7, self.t3.at[p.core], self.t3.at[p.core], p.to_core)]
+
+    def final(self):
+        return self.stage > 1
 
     def start(self):
-        for c in self.copies(1):
+        for c in self.copies(0):
             c.start()
         self.due = self.clock.now + 1.5
 
     def advance(self):
-        for c in self.copies(self.stage):
-            if self.stage < 3:
+        p, stage = self.p, self.stage
+        for c in self.copies(stage):
+            if stage < 2:
                 c.wait()
             else:
                 c.wait_send()
-        if self.stage == 1:
-            self.t1[...] = self.t0[...] + self.r0[...]
-        elif self.stage == 2:
-            self.r2[self.p.z] = (self.t1[...] + self.r1[0]) + (self.r1[1] + self.r1[2])
+        if stage == 0:
+            self.t1[...] = self.t0[p.core] + self.r0[...]
+        elif stage == 1:
+            self.r2[p.z] = (self.t1[...] + self.r1[0]) + (self.r1[1] + self.r1[2])
+        elif stage == 2:
+            for k in range(3):
+                there = (p.z + 3 - k) % 4
+                self.copy(4 + k, self.r2.at[there], self.r2.at[there], p.to_z[k]).wait_recv()
+            self.t3[p.core] = (self.r2[0] + self.r2[1]) + (self.r2[2] + self.r2[3])
         else:
-            for k in range(3):
-                there = (self.p.z + 3 - k) % 4
-                self.copy(4 + k, self.r2.at[there], self.r2.at[there], self.p.to_z[k]).wait_recv()
-            self.finish((self.r2[0] + self.r2[1]) + (self.r2[2] + self.r2[3]))
-        if self.stage < 3:
-            for c in self.copies(self.stage + 1):
+            self.copy(7, self.t3.at[1 - p.core], self.t3.at[1 - p.core], p.to_core).wait_recv()
+            self.finish(self.t3)
+        self.stage += 1
+        if self.stage < 4:
+            for c in self.copies(self.stage):
                 c.start()
-            self.due = self.clock.arrival(self.stage, 4 * self.size) + 0.5
-        self.stage += 1
+            if self.stage == 3:
+                self.due = self.clock.now + 1.5
+            else:
+                self.due = self.clock.arrival(("xy", "z")[self.stage - 1], 4 * self.size) + (2.0 if self.stage == 1 else 0.5)
 
 
 def kernel(dims, names, *all_refs):
@@ -265,12 +341,13 @@
         for u in range(unroll):
             j = i * unroll + u
             found = dot(both, one_hot(j))
-            bias_rows[pl.ds(pl.multiple_of(j * heads, heads), heads), :] = (
+            bias_rows[j * heads : (j + 1) * heads, :] = (
                 found[:heads] + found[heads:]
             ) * LOG2E
         return carry
 
-    lax.fori_loop(0, count // unroll, look, 0)
+    for i in range(count // unroll):
+        look(i, 0)
     for g in range(groups):
         bias[g] = jnp.concatenate(
             [bias_rows[pl.ds(g * GROUP + h, PAD, stride=heads), :][:, :PAD] for h in range(GROUP)],
@@ -359,33 +436,35 @@
     clock = Clock()
     active = []
 
-    def put(value, ref):
+    def put(value, ref, z_first):
         for d in range(value.shape[0] // 16):
             dx, dz, dy, dc = d // 16, (d // 4) % 4, (d // 2) % 2, d % 2
             for half in range(2):
                 a, b = (dx, dy) if half == 0 else (dy, dx)
-                ref[dc, half, a, b, dz] = value[16 * d + 8 * half : 16 * d + 8 * half + 8]
+                at = (dc, dz, half, a, b) if z_first else (dc, half, a, b, dz)
+                ref[at] = value[16 * d + 8 * half : 16 * d + 8 * half + 8]
 
     def update(out, at, tiles, value):
         for half in range(2):
-            for n in range(value.shape[2] // 128):
+            for n in range(value[half].shape[1] // 128):
                 rows = pl.ds(half * 8 * tiles + at(n), 8, stride=tiles)
-                out[rows, :] = value[half, :, n * 128 : n * 128 + 128]
+                out[rows, :] = value[half][:, n * 128 : n * 128 + 128]
 
     def ship(name, n, value, finish):
         refs = [r[f"{name}_{k}"] for k in ("buf", "r0", "r1", "r2", "s2", "r3")]
-        put(value, refs[0])
-        chunk = Chunk(place, refs, r["send"].at[n], r["recv"].at[n], clock, finish)
+        z_first = name[0] == "v"
+        put(value, refs[0], z_first)
+        chunk = (ChunkZ if z_first else Chunk)(place, refs, r["send"].at[n], r["recv"].at[n], clock, finish)
         chunk.start()
         active.append(chunk)
 
     def run_due(passed, last=False):
         clock.now += passed
         while True:
-            ready = [k for k in active if k.stage < 4 and (last or k.stage < 3 and k.due <= clock.now)]
+            ready = [k for k in active if k.stage < 4 and (last or k.due <= clock.now and not k.final())]
             if not ready:
                 return
-            first = min(ready, key=lambda k: (k.stage == 3, k.due))
+            first = min(ready, key=lambda k: (k.final(), k.due))
             clock.now = max(clock.now, first.due)
             first.advance()
 
@@ -409,7 +488,7 @@
                 run_due(1.4)
         pipelined(batches, (get_scores, get_probs, use_probs), after)
         cols = slice(2 * n * wide, 2 * (n + 1) * wide)
-        g_v = dot(xt[...], d_v[:, cols])
+        g_v = tall_dot(xt, d_v[:, cols])
         if remote:
             at = lambda k, n=n: 2 * tiles + 2 * n * per + k
             ship(f"v{n}", n, g_v, functools.partial(update, r["out_qkv"], at, 3 * tiles))
@@ -418,7 +497,7 @@
             r["out_qkv"][:, 2 * dim + cols.start : 2 * dim + cols.stop] = g_v
     for n in range(2):
         cols = slice(n * half, (n + 1) * half)
-        g_proj = dot(att_t[...], c[:, cols])
+        g_proj = tall_dot(att_t, c[:, cols])
         if remote:
             at = lambda k, n=n: n * tiles // 2 + k
             ship(f"p{n}", pairs + n, g_proj, functools.partial(update, r["out_proj"], at, tiles))
@@ -452,7 +531,7 @@
             d_qk[g % 2, rows, :] = jnp.concatenate([d_q, d_k], axis=1).astype(BF16)
 
     def send_qk(g):
-        g_qk = dot(xt[...], d_qk[g % 2])
+        g_qk = tall_dot(xt, d_qk[g % 2])
         if remote:
             at = lambda n, g=g: (n // per) * tiles + g * per + n % per
             ship(f"k{g}", pairs + 2 + g, g_qk, functools.partial(update, r["out_qkv"], at, 3 * tiles))
@@ -494,19 +573,22 @@
         run_due(0.3)
     g_table = jnp.zeros((2 * heads, size), F32)
     steps = count // unroll
-    for k in range(2):
-        g_table = lax.fori_loop(k * steps // 2, (k + 1) * steps // 2, collect, g_table)
+    parts = 4
+    for k in range(parts):
+        g_table = lax.fori_loop(k * steps // parts, (k + 1) * steps // parts, collect, g_table)
         if remote:
-            run_due(0.9)
+            run_due(2.2 / parts)
     g_table = g_table[:heads] + g_table[heads:]
     if not remote:
         r["out_table"][...] = g_table[:, :entries]
         return
-    refs = [r[f"t_{k}"] for k in ("t0", "r0", "t1", "r1", "r2")]
-    refs[0][...] = g_table
+    refs = [r[f"t_{k}"] for k in ("t0", "r0", "t1", "r1", "r2", "t3")]
+    for k in range(2):
+        refs[0][k] = g_table[k * heads // 2 : (k + 1) * heads // 2]
 
     def table_done(value):
-        r["out_table"][...] = value[:, :entries]
+        for k in range(2):
+            r["out_table"][k * heads // 2 : (k + 1) * heads // 2, :] = value[k, :, :entries]
 
     n = pairs + 2 + groups
     last = Table(place, refs, r["send"].at[n], r["recv"].at[n], clock, table_done)
@@ -567,14 +649,22 @@
         chunks = {f"v{n}": 2 * wide for n in range(groups // 2)} | dict(p0=dim // 2, p1=dim // 2)
         chunks |= {f"k{g}": 2 * wide for g in range(groups)}
         for name, cols in chunks.items():
+            if name[0] == "v":
+                scratch[f"{name}_buf"] = vmem((2, 4, 2, 2, 2, 8, cols), F32)
+                scratch[f"{name}_r0"] = vmem((4, 2, 2, 2, 8, cols), F32)
+                scratch[f"{name}_r1"] = vmem((3, 2, 2, 2, 8, cols), F32)
+                scratch[f"{name}_r2"] = vmem((2, 2, 8, cols), F32)
+                scratch[f"{name}_s2"] = vmem((2, 2, 2, 8, cols), F32)
+                scratch[f"{name}_r3"] = vmem((2, 8, cols), F32)
+                continue
             scratch[f"{name}_buf"] = vmem((2, 2, 2, 2, 4, 8, cols), F32)
             scratch[f"{name}_r0"] = vmem((2, 2, 2, 4, 8, cols), F32)
             scratch[f"{name}_r1"] = vmem((2, 2, 4, 8, cols), F32)
             scratch[f"{name}_r2"] = vmem((2, 4, 8, cols), F32)
             scratch[f"{name}_s2"] = vmem((4, 2, 8, cols), F32)
             scratch[f"{name}_r3"] = vmem((3, 2, 8, cols), F32)
-        for name, lead in dict(t0=(), r0=(), t1=(), r1=(3,), r2=(4,)).items():
-            scratch[f"t_{name}"] = vmem((*lead, heads, size), F32)
+        for name, lead in dict(t0=(2,), r0=(), t1=(), r1=(3,), r2=(4,), t3=(2,)).items():
+            scratch[f"t_{name}"] = vmem((*lead, heads // 2, size), F32)
         scratch["send"] = pltpu.SemaphoreType.DMA((len(chunks) + 1, COPIES))
         scratch["recv"] = pltpu.SemaphoreType.DMA((len(chunks) + 1, COPIES))
         params = dict(collective_id=0, has_side_effects=True)

time: 47 us -> 43.9 us (0.934)
  Pallas kernels: 46.1 us -> 43 us
    pallas_call x1, Pallas kernels: 44.5 us -> 41.4 us  [local_grads(): pl.pallas_call(functools.partial(kernel, dims, [*inputs, *outs, *scratch]...]
where the time goes in v3:
time: 43.9 us; the launch traced here: 43.6 us
  Pallas kernels  43 us (98%)
  between operations  0.64 us (1%)
    pallas_call x1, Pallas kernels, local_grads(): pl.pallas_call(functools.partial(kernel, dims, [*inputs, *outs, *scratch]...  41.4 us
    pallas_call x1, Pallas kernels, momentum(): pl.pallas_call(functools.partial(momentum_kernel, norm), out_shape=[jax.S...  1.63 us

profile of v3, /device:TPU:0, one launch (start us, length us, event | category | flops | bytes accessed | tf_op | source)
XLA Modules:
  0.0 43.6 jit_solution(4012659608021906469)
XLA Ops:
  0.6 41.4 %shard_map.121 = (f32[192,128]{1,0:T(8,128)}, f32[64,128]{1,0:T(8,128)}, f32[16,169]{1,0:T(8,128)}) custom-call(s32[16,49]{1,0:T(8,128)} %all_refs_0_.1, s32[49,49]{1,0:T(8,128)} %all_refs_1_.1, f32[16,169]{1,0:T(8,128)} %bitcast.13, bf16[49,16,512]{2,1,0:T(8,128)(2,1)} %bitcast.9, bf16[512,1536]{1,0:T(8,128)(2,1)} %all_refs_4_.1, ...), custom_call_target="tpu_custom_call" | custom-call | tf_op jit(solution)/shard_map/pallas_call | solution.py:673
  42.0 1.6 %shard_map.122 = (f32[192,128]{1,0:T(8,128)}, f32[64,128]{1,0:T(8,128)}, f32[16,169]{1,0:T(8,128)}) custom-call(f32[192,128]{1,0:T(8,128)} %get-tuple-element.9.refs_0_, f32[64,128]{1,0:T(8,128)} %get-tuple-element.10.refs_1_, f32[16,169]{1,0:T(8,128)} %get-tuple-element.11.refs_2_, f32[192,128]{1,0:T(8,128)} %bitcast.11, f32[64,128]{1,0:T(8,128)} %bitcast.12, ...), custom_call_target="tpu_custom_call" | custom-call | tf_op jit(solution)/shard_map/pallas_call | solution.py:691
